TPU v7x, 32 devices: a whole 2x2x4 slice. The times are simulated.
32 devices in a mesh: patch: 8 (over y, x, core), rhs: 4 (over z).
Axes of the slice: x: 2, y: 2, z: 4, core: 2. Of those that a mesh axis runs over, the one named last changes fastest.
Arguments:
- rhs_vectors: float32 [64, 16, 384], P('patch', 'rhs'), may hold values from -8 to 8
- near_blocks: bfloat16 [64, 4, 384, 384], P('patch'), may hold values from -1 to 5, as said below
- neighbours: int32 [64, 4], P('patch'), may hold values from 0 to 63, as said below
- up_maps: float32 [64, 64, 384], P('patch'), may hold values from -0.3125 to 0.3125
- shift_up: float32 [64, 64, 64], P('patch'), may hold values from -0.25 to 0.25
- far_lists: int32 [8, 4], P('patch'), may hold values from 0 to 7, as said below
- translations: float32 [8, 4, 64, 64], P('patch'), may hold values from -0.375 to 0.375
- shift_down: float32 [64, 64, 64], P('patch'), may hold values from -0.75 to 0.75
- down_maps: float32 [64, 384, 64], P('patch'), may hold values from -0.375 to 0.375
Outputs:
- solution: float32 [64, 16, 384], P('patch', 'rhs')
- residual: float32 [64, 16, 384], P('patch', 'rhs')
Inputs may be any that keep to these rules, and one draw needn't show every extreme that they name: `neighbours`: entry 0 of each row is the patch itself; every other entry names a patch of the same cell or of the cell just before or just after it, cyclically. `far_lists`: entry 0 of each row names the cell just before or just after the row's own cell, cyclically, and for cell 0 the cell just before it; every other entry names a cell other than the row's own. `near_blocks`: the blocks keep the operator's symmetric part positive definite.
All inputs are finite; a program needn't handle non-finite values.
Results may differ from a plain program's by a relative error of at most 0.008.
The roundings to bfloat16 on the way count: a program that leaves them out, or rounds other values in their place, can miss the bound.
Values may be sent and summed in bfloat16 or wider, within the bound.
A program may use at most 64 MiB of HBM per device.

v0:
```python
import jax
import jax.numpy as jnp
from jax import lax
from jax.sharding import PartitionSpec as P

ITERS = 2
HIGH = lax.Precision.HIGHEST


def with_halo(block, sides, width):
    for axis, dim in sides:
        count = lax.axis_size(axis)
        forward = [(i, i + 1) for i in range(count - 1)]
        forward.append((count - 1, 0))
        backward = [(target, source) for source, target in forward]
        low = lax.ppermute(
            lax.slice_in_dim(block, block.shape[dim] - width, None, axis=dim), axis, forward
        )
        high = lax.ppermute(lax.slice_in_dim(block, 0, width, axis=dim), axis, backward)
        block = jnp.concatenate([low, block, high], axis=dim)
    return block


def spd_solve(matrix, right):
    factor = jnp.linalg.cholesky(matrix)
    return jax.scipy.linalg.cho_solve((factor, True), right)


def gram(left, right):
    return jnp.einsum("pkw,plw->kl", left, right, precision=HIGH)


def mix(field, coeffs):
    return jnp.einsum("pkw,kl->plw", field, coeffs, precision=HIGH)


def residual_sum(residual):
    return lax.psum(gram(residual, residual), "patch")


def apply_operator(
    field,
    near_blocks,
    neighbours,
    up_maps,
    shift_up,
    far_lists,
    translations,
    shift_down,
    down_maps,
):
    patches = field.shape[0]
    count = lax.axis_size("patch")
    first = lax.axis_index("patch") * patches - patches
    rounded = field.astype(jnp.bfloat16)
    widened = with_halo(rounded, (("patch", 0),), patches)
    local_ids = jnp.mod(neighbours - first, patches * count)
    picked = widened[local_ids]
    near = jnp.einsum("pjvw,pjkw->pkv", near_blocks, picked, preferred_element_type=jnp.float32)
    moments = jnp.einsum("pew,pkw->pke", up_maps, field, precision=HIGH)
    cell_moment = jnp.einsum("pfe,pke->kf", shift_up, moments, precision=HIGH)
    sources = far_lists[0]
    table = translations[0]
    piece = lax.all_gather(cell_moment[None], "patch", axis=0, tiled=True)
    labels = jnp.arange(piece.shape[0], dtype=jnp.int32)
    select = (sources[:, None] == labels[None, :]).astype(jnp.float32)
    chosen = jnp.einsum("ji,ike->jke", select, piece, precision=HIGH)
    local_exp = jnp.zeros_like(cell_moment) + jnp.einsum(
        "jfe,jke->kf", table, chosen, precision=HIGH
    )
    patch_exp = jnp.einsum("pfe,ke->pkf", shift_down, local_exp, precision=HIGH)
    far = jnp.einsum("pvf,pkf->pkv", down_maps, patch_exp, precision=HIGH)
    return near + far


def on_device(
    rhs_vectors,
    near_blocks,
    neighbours,
    up_maps,
    shift_up,
    far_lists,
    translations,
    shift_down,
    down_maps,
):
    my_cols = rhs_vectors.shape[1]
    offset = lax.axis_index("rhs") * my_cols
    residual = lax.all_gather(rhs_vectors, "rhs", axis=1, tiled=True)
    solution = jnp.zeros_like(residual)
    direction = residual
    current = jnp.zeros((residual.shape[1], residual.shape[1]), jnp.float32)
    for step in range(ITERS):
        image = apply_operator(
            direction,
            near_blocks,
            neighbours,
            up_maps,
            shift_up,
            far_lists,
            translations,
            shift_down,
            down_maps,
        )
        if step == 0:
            current = residual_sum(residual)
        curve = lax.psum(gram(direction, image), "patch")
        curve = 0.5 * (curve + curve.T)
        alpha = spd_solve(curve, current)
        solution = solution + mix(direction, alpha)
        residual = residual - mix(image, alpha)
        if step + 1 < ITERS:
            following = residual_sum(residual)
            beta = spd_solve(current, following)
            direction = residual + mix(direction, beta)
            current = following
    solution_mine = lax.dynamic_slice_in_dim(solution, offset, my_cols, 1)
    residual_mine = lax.dynamic_slice_in_dim(residual, offset, my_cols, 1)
    return (solution_mine, residual_mine)


def solution(mesh):
    return jax.shard_map(
        on_device,
        mesh=mesh,
        in_specs=(
            P("patch", "rhs", None),
            P("patch", None, None, None),
            P("patch", None),
            P("patch", None, None),
            P("patch", None, None),
            P("patch", None),
            P("patch", None, None, None),
            P("patch", None, None),
            P("patch", None, None),
        ),
        out_specs=(P("patch", "rhs", None), P("patch", "rhs", None)),
        check_vma=False,
    )
```

profile of v0, /device:TPU:0, one launch (start us, length us, event | category | flops | bytes accessed | tf_op | source)
XLA Modules:
  0.0 129.5 jit_solution(5300560113778208520)
XLA Ops:
  0.6 0.9 copy.61
  1.5 15.5 %all_gather.9 = f32[8,16,384]{2,0,1:T(8,128)S(1)} all-gather(f32[8,4,384]{2,0,1:T(8,128)S(1)} %copy.61), channel_id=1, replica_groups=mesh['patch'=8,'rhs'=4] {'rhs'}, dimensions={1}, use_global_device_ids=true | all-gather | bytes 245760 | tf_op jit(solution)/shard_map/all_gather | solution.py:89
  17.9 0.7 compare_select_fusion
  18.8 2.1 %fusion.11 = f32[8,16,64]{2,1,0:T(8,128)S(1)} fusion(f32[8,64,384]{2,1,0:T(8,128)} %param.15, f32[8,16,384]{2,0,1:T(8,128)S(1)} %all_gather.9), kind=kOutput, calls=%fused_computation.33 | convolution fusion | flops 37748736 | bytes 1015808 | tf_op jit(solution)/shard_map/pew,pkw->pke/dot_general | solution.py:60
  20.9 1.2 convolution_bitcast_fusion.11
  22.1 9.3 %all-gather = f32[128,64]{1,0:T(8,128)S(1)} all-gather(f32[16,64]{1,0:T(8,128)S(1)} %convolution_bitcast_fusion.11), channel_id=2, replica_groups=mesh['patch'=8,'rhs'=4] {'patch'}, dimensions={0}, use_global_device_ids=true | all-gather | bytes 36864 | tf_op jit(solution)/shard_map/all_gather | solution.py:64
  31.4 0.9 fusion.15
  32.3 1.1 fusion.4
  33.4 1.7 %convolution_bitcast_fusion.6 = f32[8,16,64]{2,1,0:T(8,128)S(1)} fusion(f32[16,64,1]{1,0,2:T(8,128)S(1)} %fusion.4, f32[8,64,64]{2,1,0:T(8,128)} %param.19), kind=kOutput, calls=%fused_computation.12 | convolution fusion | flops 6291456 | bytes 167936 | tf_op jit(solution)/shard_map/pfe,ke->pkf/dot_general | solution.py:71
  35.9 6.3 %convolution_bitcast_fusion.4 = f32[8,16,384]{2,1,0:T(8,128)S(1)} fusion(bf16[8,4,16,384]{3,2,1,0:T(8,128)(2,1)S(1)} %bitcast.140, bf16[8,4,384,384]{3,2,1,0:T(8,128)(2,1)} %param.13), kind=kOutput, calls=%fused_computation.10 | convolution fusion | flops 150994944 | bytes 10027008 | tf_op jit(solution)/shard_map/pjvw,pjkw->pkv/dot_general | solution.py:59
  43.2 23.6 %all-reduce = (f32[16,16]{0,1:T(8,128)S(1)}, f32[16,16]{1,0:T(8,128)S(1)}) all-reduce(f32[16,16]{0,1:T(8,128)S(1)} %convolution_bitcast_fusion.14, f32[16,16]{1,0:T(8,128)S(1)} %convolution_bitcast_fusion.15), channel_id=1, replica_groups=mesh['patch'=8,'rhs'=4] {'patch'}, use_global_device_ids=true, to_apply=%region_3.5 | all-reduce | flops 512 | bytes 4096 | tf_op jit(solution)/shard_map/psum | solution.py:38
  67.0 1.5 %cholesky.59 = f32[16,16]{1,0:T(8,128)S(1)} custom-call(f32[16,16]{1,0:T(8,128)S(1)} %fusion.35), custom_call_target="Cholesky" | custom-call | tf_op jit(solution)/shard_map/jit(cholesky)/cholesky | solution.py:25
  69.1 0.6 fusion.20
  69.8 1.2 custom-call.9
  72.1 12.1 %psum.30 = f32[16,16]{1,0:T(8,128)S(1)} all-reduce(f32[16,16]{1,0:T(8,128)S(1)} %convolution_bitcast_fusion.13), channel_id=1, replica_groups=mesh['patch'=8,'rhs'=4] {'patch'}, use_global_device_ids=true, to_apply=%region_4.7 | all-reduce | flops 256 | bytes 2048 | tf_op jit(solution)/shard_map/psum | solution.py:38
  84.2 1.4 %cholesky.70 = f32[16,16]{1,0:T(8,128)S(1)} custom-call(f32[16,16]{1,0:T(8,128)S(1)} %fusion.31), custom_call_target="Cholesky" | custom-call | tf_op jit(solution)/shard_map/jit(cholesky)/cholesky | solution.py:25
  87.0 1.2 custom-call.10
  89.8 0.9 fusion.44
  91.1 9.4 %all-gather.1 = f32[128,64]{1,0:T(8,128)S(1)} all-gather(f32[16,64]{1,0:T(8,128)S(1)} %convolution_bitcast_fusion.8), channel_id=3, replica_groups=mesh['patch'=8,'rhs'=4] {'patch'}, dimensions={0}, use_global_device_ids=true | all-gather | bytes 36864 | tf_op jit(solution)/shard_map/all_gather | solution.py:64
  100.9 0.7 convolution_bitcast_fusion.5
  102.3 6.2 %convolution_bitcast_fusion.3 = f32[8,16,384]{2,1,0:T(8,128)S(1)} fusion(bf16[8,4,16,384]{3,2,1,0:T(8,128)(2,1)S(1)} %bitcast.139, bf16[8,4,384,384]{3,2,1,0:T(8,128)(2,1)} %param.13), kind=kOutput, calls=%fused_computation.9 | convolution fusion | flops 150994944 | bytes 10027008 | tf_op jit(solution)/shard_map/pjvw,pjkw->pkv/dot_general | solution.py:59
  109.5 13.5 %psum.31 = f32[16,16]{1,0:T(8,128)S(1)} all-reduce(f32[16,16]{1,0:T(8,128)S(1)} %convolution_bitcast_fusion.12), channel_id=1, replica_groups=mesh['patch'=8,'rhs'=4] {'patch'}, use_global_device_ids=true, to_apply=%region_5.8 | all-reduce | flops 256 | bytes 2048 | tf_op jit(solution)/shard_map/psum | solution.py:107
  123.1 1.5 %cholesky.81 = f32[16,16]{1,0:T(8,128)S(1)} custom-call(f32[16,16]{1,0:T(8,128)S(1)} %fusion.26), custom_call_target="Cholesky" | custom-call | tf_op jit(solution)/shard_map/jit(cholesky)/cholesky | solution.py:25
  125.9 1.2 custom-call.11
  (68 shorter events, 13.9 us)
Async XLA Ops:
  0.6 41.6 %copy-start = (f32[8,384,64]{1,2,0:T(8,128)S(1)}, f32[8,384,64]{1,2,0:T(8,128)}, u32[]{:S(2)}) copy-start(f32[8,384,64]{1,2,0:T(8,128)} %param.20) | copy-start | bytes 2359300
  17.0 18.1 %collective-permute-start.1 = (bf16[8,16,384]{2,1,0:T(8,128)(2,1)S(1)}, bf16[8,16,384]{2,1,0:T(8,128)(2,1)S(1)}, u32[]{:S(2)}, u32[]{:S(2)}) collective-permute-start(bf16[8,16,384]{2,1,0:T(8,128)(2,1)S(1)} %copy.116), channel_id=1, source_target_pairs={{4,0},{8,4},{12,8},{16,12},{20,16},{24,20},{28,24},{0,28},{5,1},{9... | collective-permute-start | bytes 294920 | tf_op jit(solution)/shard_map/ppermute | solution.py:19
  17.1 18.1 %collective-permute-start = (bf16[8,16,384]{2,1,0:T(8,128)(2,1)S(1)}, bf16[8,16,384]{2,1,0:T(8,128)(2,1)S(1)}, u32[]{:S(2)}, u32[]{:S(2)}) collective-permute-start(bf16[8,16,384]{2,1,0:T(8,128)(2,1)S(1)} %copy.116), channel_id=1, source_target_pairs={{0,4},{4,8},{8,12},{12,16},{16,20},{20,24},{24,28},{28,0},{1,5},{5... | collective-permute-start | bytes 294920 | tf_op jit(solution)/shard_map/ppermute | solution.py:16
  35.8 54.0 %copy-start.1 = (f32[8,64,384]{2,1,0:T(8,128)S(1)}, f32[8,64,384]{2,1,0:T(8,128)}, u32[]{:S(2)}) copy-start(f32[8,64,384]{2,1,0:T(8,128)} %param.15) | copy-start | bytes 2359300
  35.9 54.9 %copy-start.2 = (f32[8,64,64]{2,1,0:T(8,128)S(1)}, f32[8,64,64]{2,1,0:T(8,128)}, u32[]{:S(2)}) copy-start(f32[8,64,64]{2,1,0:T(8,128)} %param.16) | copy-start | bytes 393220
  35.9 64.6 %copy-start.5 = (s32[1,4]{1,0:T(1,128)S(1)}, s32[1,4]{1,0:T(1,128)}, u32[]{:S(2)}) copy-start(s32[1,4]{1,0:T(1,128)} %param.17) | copy-start | bytes 52
  35.9 64.8 %copy-start.4 = (f32[1,4,64,64]{3,2,1,0:T(8,128)S(1)}, f32[1,4,64,64]{3,2,1,0:T(8,128)}, u32[]{:S(2)}) copy-start(f32[1,4,64,64]{3,2,1,0:T(8,128)} %param.18) | copy-start | bytes 196612
  35.9 65.0 %copy-start.3 = (f32[8,64,64]{2,1,0:T(8,128)S(1)}, f32[8,64,64]{2,1,0:T(8,128)}, u32[]{:S(2)}) copy-start(f32[8,64,64]{2,1,0:T(8,128)} %param.19) | copy-start | bytes 393220
  89.0 12.6 %collective-permute-start.3 = (bf16[8,16,384]{2,1,0:T(8,128)(2,1)S(1)}, bf16[8,16,384]{2,1,0:T(8,128)(2,1)S(1)}, u32[]{:S(2)}, u32[]{:S(2)}) collective-permute-start(bf16[8,16,384]{2,1,0:T(8,128)(2,1)S(1)} %get-tuple-element.6), channel_id=1, source_target_pairs={{4,0},{8,4},{12,8},{16,12},{20,16},{24,20},{28,24},{0,28},{5,1},{9... | collective-permute-start | bytes 294920 | tf_op jit(solution)/shard_map/ppermute | solution.py:19
  89.0 12.6 %collective-permute-start.2 = (bf16[8,16,384]{2,1,0:T(8,128)(2,1)S(1)}, bf16[8,16,384]{2,1,0:T(8,128)(2,1)S(1)}, u32[]{:S(2)}, u32[]{:S(2)}) collective-permute-start(bf16[8,16,384]{2,1,0:T(8,128)(2,1)S(1)} %get-tuple-element.6), channel_id=1, source_target_pairs={{0,4},{4,8},{8,12},{12,16},{16,20},{20,24},{24,28},{28,0},{1,5},{5... | collective-permute-start | bytes 294920 | tf_op jit(solution)/shard_map/ppermute | solution.py:16
where the time goes:
time: 130 us; the launch traced here: 129 us
  blocking collectives  83.3 us (64%)
  matrix products  27.2 us (21%)
  other arithmetic  14.2 us (11%)
  local copies, waits for them, and re-layouts  2.76 us (2%)
    psum x2, blocking collectives, residual_sum(): return lax.psum(gram(residual, residual), 'patch')  35.7 us
    all_gather x2, blocking collectives, apply_operator(): piece = lax.all_gather(cell_moment[None], 'patch', axis=0, tiled=True)  18.7 us
    all_gather x1, blocking collectives, on_device(): residual = lax.all_gather(rhs_vectors, 'rhs', axis=1, tiled=True)  15.5 us
    psum x1, blocking collectives, on_device(): curve = lax.psum(gram(direction, image), 'patch')  13.5 us
    dot_general x2, matrix products, apply_operator(): jnp.einsum('pjvw,pjkw->pkv', near_blocks, picked, preferred_element_type=...  12.5 us
    another operation x9, other arithmetic, spd_solve(): factor = jnp.linalg.cholesky(matrix)  6.39 us
    another operation x6, other arithmetic, spd_solve(): return jax.scipy.linalg.cho_solve((factor, True), right)  5.63 us
    dot_general x2, matrix products, apply_operator(): moments = jnp.einsum('pew,pkw->pke', up_maps, field, precision=HIGH)  2.99 us
  transfers between devices with their start and end apart: 4, of which 0 were waited for; matrix products, arithmetic and copies ran while one was open for 8% of the time, Pallas kernels for 0%

commit v1 on v0

--- a/solution.py
+++ b/solution.py
@@ -104,7 +104,8 @@
         )
         if step == 0:
             current = residual_sum(residual)
-        curve = lax.psum(gram(direction, image), "patch")
+        set_slices_on = lambda a0: jnp.sum(lax.all_gather(a0, "patch"), 0)
+        curve = set_slices_on(gram(direction, image))
         curve = 0.5 * (curve + curve.T)
         alpha = spd_solve(curve, current)
         solution = solution + mix(direction, alpha)

time: 130 us -> 126 us (0.969)
  blocking collectives: 83.3 us -> 78.9 us
    all_gather x0 -> x2, blocking collectives: none -> 17.1 us  [on_device(): set_slices_on = lambda a0: jnp.sum(lax.all_gather(a0, 'patch'), 0)]
    psum x1 -> x0, blocking collectives: 13.5 us -> none  [on_device(): curve = lax.psum(gram(direction, image), 'patch')]
    psum x2, blocking collectives: 35.7 us -> 27.7 us  [residual_sum(): return lax.psum(gram(residual, residual), 'patch')]
  transfers between devices with their start and end apart: 4 -> 4, of which waited for: 0 -> 0; matrix products, arithmetic and copies ran while one was open for 8% -> 12% of each run, Pallas kernels for 0% -> 0%
where the time goes in v1:
time: 126 us; the launch traced here: 125 us
  blocking collectives  78.9 us (63%)
  matrix products  27.2 us (22%)
  other arithmetic  14.2 us (11%)
  local copies, waits for them, and re-layouts  2.84 us (2%)
    psum x2, blocking collectives, residual_sum(): return lax.psum(gram(residual, residual), 'patch')  27.7 us
    all_gather x2, blocking collectives, apply_operator(): piece = lax.all_gather(cell_moment[None], 'patch', axis=0, tiled=True)  18.6 us
    all_gather x2, blocking collectives, on_device(): set_slices_on = lambda a0: jnp.sum(lax.all_gather(a0, 'patch'), 0)  17.1 us
    all_gather x1, blocking collectives, on_device(): residual = lax.all_gather(rhs_vectors, 'rhs', axis=1, tiled=True)  15.5 us
    dot_general x2, matrix products, apply_operator(): jnp.einsum('pjvw,pjkw->pkv', near_blocks, picked, preferred_element_type=...  12.5 us
    another operation x9, other arithmetic, spd_solve(): factor = jnp.linalg.cholesky(matrix)  6.39 us
    another operation x6, other arithmetic, spd_solve(): return jax.scipy.linalg.cho_solve((factor, True), right)  5.63 us
    dot_general x2, matrix products, apply_operator(): moments = jnp.einsum('pew,pkw->pke', up_maps, field, precision=HIGH)  2.99 us
  transfers between devices with their start and end apart: 4, of which 0 were waited for; matrix products, arithmetic and copies ran while one was open for 12% of the time, Pallas kernels for 0%

profile of v1, /device:TPU:0, one launch (start us, length us, event | category | flops | bytes accessed | tf_op | source)
XLA Modules:
  0.0 125.2 jit_solution(2006733811853276596)
XLA Ops:
  0.6 0.9 copy.60
  1.5 15.5 %all_gather.21 = f32[8,16,384]{2,0,1:T(8,128)S(1)} all-gather(f32[8,4,384]{2,0,1:T(8,128)S(1)} %copy.60), channel_id=1, replica_groups=mesh['patch'=8,'rhs'=4] {'rhs'}, dimensions={1}, use_global_device_ids=true | all-gather | bytes 245760 | tf_op jit(solution)/shard_map/all_gather | solution.py:89
  17.9 14.3 %psum.14 = f32[16,16]{0,1:T(8,128)S(1)} all-reduce(f32[16,16]{0,1:T(8,128)S(1)} %convolution_bitcast_fusion.14), channel_id=1, replica_groups=mesh['patch'=8,'rhs'=4] {'patch'}, use_global_device_ids=true, to_apply=%region_3.5 | all-reduce | flops 256 | bytes 2048 | tf_op jit(solution)/shard_map/psum | solution.py:38
  32.2 0.7 compare_select_fusion
  33.1 2.1 %fusion.11 = f32[8,16,64]{2,1,0:T(8,128)S(1)} fusion(f32[8,64,384]{2,1,0:T(8,128)} %param.15, f32[8,16,384]{2,0,1:T(8,128)S(1)} %all_gather.21), kind=kOutput, calls=%fused_computation.33 | convolution fusion | flops 37748736 | bytes 1015808 | tf_op jit(solution)/shard_map/pew,pkw->pke/dot_general | solution.py:60
  35.1 1.2 convolution_bitcast_fusion.11
  36.4 9.3 %all-gather = f32[128,64]{1,0:T(8,128)S(1)} all-gather(f32[16,64]{1,0:T(8,128)S(1)} %convolution_bitcast_fusion.11), channel_id=2, replica_groups=mesh['patch'=8,'rhs'=4] {'patch'}, dimensions={0}, use_global_device_ids=true | all-gather | bytes 36864 | tf_op jit(solution)/shard_map/all_gather | solution.py:64
  45.7 1.5 %cholesky.70 = f32[16,16]{1,0:T(8,128)S(1)} custom-call(f32[16,16]{1,0:T(8,128)S(1)} %fusion.31), custom_call_target="Cholesky" | custom-call | tf_op jit(solution)/shard_map/jit(cholesky)/cholesky | solution.py:25
  48.5 1.2 custom-call.10
  49.8 0.9 fusion.15
  50.6 1.1 fusion.4
  51.7 1.7 %convolution_bitcast_fusion.6 = f32[8,16,64]{2,1,0:T(8,128)S(1)} fusion(f32[16,64,1]{1,0,2:T(8,128)S(1)} %fusion.4, f32[8,64,64]{2,1,0:T(8,128)} %param.19), kind=kOutput, calls=%fused_computation.12 | convolution fusion | flops 6291456 | bytes 167936 | tf_op jit(solution)/shard_map/pfe,ke->pkf/dot_general | solution.py:71
  54.2 6.3 %convolution_bitcast_fusion.4 = f32[8,16,384]{2,1,0:T(8,128)S(1)} fusion(bf16[8,4,16,384]{3,2,1,0:T(8,128)(2,1)S(1)} %bitcast.142, bf16[8,4,384,384]{3,2,1,0:T(8,128)(2,1)} %param.13), kind=kOutput, calls=%fused_computation.10 | convolution fusion | flops 150994944 | bytes 10027008 | tf_op jit(solution)/shard_map/pjvw,pjkw->pkv/dot_general | solution.py:59
  61.6 8.3 %all-gather.1 = f32[128,16]{1,0:T(8,128)S(1)} all-gather(f32[16,16]{1,0:T(8,128)S(1)} %copy.67), channel_id=3, replica_groups=mesh['patch'=8,'rhs'=4] {'patch'}, dimensions={0}, use_global_device_ids=true | all-gather | bytes 9216 | tf_op jit(solution)/shard_map/all_gather | solution.py:107
  70.1 1.5 %cholesky.59 = f32[16,16]{1,0:T(8,128)S(1)} custom-call(f32[16,16]{1,0:T(8,128)S(1)} %fusion.35), custom_call_target="Cholesky" | custom-call | tf_op jit(solution)/shard_map/jit(cholesky)/cholesky | solution.py:25
  72.9 1.2 custom-call.9
  75.2 13.5 %psum.15 = f32[16,16]{1,0:T(8,128)S(1)} all-reduce(f32[16,16]{1,0:T(8,128)S(1)} %convolution_bitcast_fusion.13), channel_id=1, replica_groups=mesh['patch'=8,'rhs'=4] {'patch'}, use_global_device_ids=true, to_apply=%region_4.7 | all-reduce | flops 256 | bytes 2048 | tf_op jit(solution)/shard_map/psum | solution.py:38
  90.2 0.9 fusion.44
  91.5 9.3 %all-gather.2 = f32[128,64]{1,0:T(8,128)S(1)} all-gather(f32[16,64]{1,0:T(8,128)S(1)} %convolution_bitcast_fusion.8), channel_id=4, replica_groups=mesh['patch'=8,'rhs'=4] {'patch'}, dimensions={0}, use_global_device_ids=true | all-gather | bytes 36864 | tf_op jit(solution)/shard_map/all_gather | solution.py:64
  101.2 0.7 convolution_bitcast_fusion.5
  102.7 6.2 %convolution_bitcast_fusion.3 = f32[8,16,384]{2,1,0:T(8,128)S(1)} fusion(bf16[8,4,16,384]{3,2,1,0:T(8,128)(2,1)S(1)} %bitcast.141, bf16[8,4,384,384]{3,2,1,0:T(8,128)(2,1)} %param.13), kind=kOutput, calls=%fused_computation.9 | convolution fusion | flops 150994944 | bytes 10027008 | tf_op jit(solution)/shard_map/pjvw,pjkw->pkv/dot_general | solution.py:59
  109.8 8.9 %all-gather.3 = f32[128,16]{1,0:T(8,128)S(1)} all-gather(f32[16,16]{1,0:T(8,128)S(1)} %convolution_bitcast_fusion.12), channel_id=5, replica_groups=mesh['patch'=8,'rhs'=4] {'patch'}, dimensions={0}, use_global_device_ids=true | all-gather | bytes 9216 | tf_op jit(solution)/shard_map/all_gather | solution.py:107
  118.9 1.5 %cholesky.81 = f32[16,16]{1,0:T(8,128)S(1)} custom-call(f32[16,16]{1,0:T(8,128)S(1)} %fusion.26), custom_call_target="Cholesky" | custom-call | tf_op jit(solution)/shard_map/jit(cholesky)/cholesky | solution.py:25
  121.7 1.2 custom-call.11
  (72 shorter events, 14.6 us)
Async XLA Ops:
  0.6 59.9 %copy-start = (f32[8,384,64]{1,2,0:T(8,128)S(1)}, f32[8,384,64]{1,2,0:T(8,128)}, u32[]{:S(2)}) copy-start(f32[8,384,64]{1,2,0:T(8,128)} %param.20) | copy-start | bytes 2359300
  17.0 36.5 %collective-permute-start.1 = (bf16[8,16,384]{2,1,0:T(8,128)(2,1)S(1)}, bf16[8,16,384]{2,1,0:T(8,128)(2,1)S(1)}, u32[]{:S(2)}, u32[]{:S(2)}) collective-permute-start(bf16[8,16,384]{2,1,0:T(8,128)(2,1)S(1)} %copy.115), channel_id=1, source_target_pairs={{4,0},{8,4},{12,8},{16,12},{20,16},{24,20},{28,24},{0,28},{5,1},{9... | collective-permute-start | bytes 294920 | tf_op jit(solution)/shard_map/ppermute | solution.py:19
  17.1 36.4 %collective-permute-start = (bf16[8,16,384]{2,1,0:T(8,128)(2,1)S(1)}, bf16[8,16,384]{2,1,0:T(8,128)(2,1)S(1)}, u32[]{:S(2)}, u32[]{:S(2)}) collective-permute-start(bf16[8,16,384]{2,1,0:T(8,128)(2,1)S(1)} %copy.115), channel_id=1, source_target_pairs={{0,4},{4,8},{8,12},{12,16},{16,20},{20,24},{24,28},{28,0},{1,5},{5... | collective-permute-start | bytes 294920 | tf_op jit(solution)/shard_map/ppermute | solution.py:16
  54.2 36.1 %copy-start.1 = (f32[8,64,384]{2,1,0:T(8,128)S(1)}, f32[8,64,384]{2,1,0:T(8,128)}, u32[]{:S(2)}) copy-start(f32[8,64,384]{2,1,0:T(8,128)} %param.15) | copy-start | bytes 2359300
  54.2 37.0 %copy-start.2 = (f32[8,64,64]{2,1,0:T(8,128)S(1)}, f32[8,64,64]{2,1,0:T(8,128)}, u32[]{:S(2)}) copy-start(f32[8,64,64]{2,1,0:T(8,128)} %param.16) | copy-start | bytes 393220
  54.2 46.6 %copy-start.5 = (s32[1,4]{1,0:T(1,128)S(1)}, s32[1,4]{1,0:T(1,128)}, u32[]{:S(2)}) copy-start(s32[1,4]{1,0:T(1,128)} %param.17) | copy-start | bytes 52
  54.2 46.8 %copy-start.4 = (f32[1,4,64,64]{3,2,1,0:T(8,128)S(1)}, f32[1,4,64,64]{3,2,1,0:T(8,128)}, u32[]{:S(2)}) copy-start(f32[1,4,64,64]{3,2,1,0:T(8,128)} %param.18) | copy-start | bytes 196612
  54.2 47.0 %copy-start.3 = (f32[8,64,64]{2,1,0:T(8,128)S(1)}, f32[8,64,64]{2,1,0:T(8,128)}, u32[]{:S(2)}) copy-start(f32[8,64,64]{2,1,0:T(8,128)} %param.19) | copy-start | bytes 393220
  89.4 12.6 %collective-permute-start.3 = (bf16[8,16,384]{2,1,0:T(8,128)(2,1)S(1)}, bf16[8,16,384]{2,1,0:T(8,128)(2,1)S(1)}, u32[]{:S(2)}, u32[]{:S(2)}) collective-permute-start(bf16[8,16,384]{2,1,0:T(8,128)(2,1)S(1)} %get-tuple-element.4), channel_id=1, source_target_pairs={{4,0},{8,4},{12,8},{16,12},{20,16},{24,20},{28,24},{0,28},{5,1},{9... | collective-permute-start | bytes 294920 | tf_op jit(solution)/shard_map/ppermute | solution.py:19
  89.4 12.5 %collective-permute-start.2 = (bf16[8,16,384]{2,1,0:T(8,128)(2,1)S(1)}, bf16[8,16,384]{2,1,0:T(8,128)(2,1)S(1)}, u32[]{:S(2)}, u32[]{:S(2)}) collective-permute-start(bf16[8,16,384]{2,1,0:T(8,128)(2,1)S(1)} %get-tuple-element.4), channel_id=1, source_target_pairs={{0,4},{4,8},{8,12},{12,16},{16,20},{20,24},{24,28},{28,0},{1,5},{5... | collective-permute-start | bytes 294920 | tf_op jit(solution)/shard_map/ppermute | solution.py:16
